TPU v7x, 32 devices: a whole 2x2x4 slice. The times are simulated.
32 devices in a mesh: pole: 2 (over y), leaf: 16 (over z, x, core).
Axes of the slice: x: 2, y: 2, z: 4, core: 2. Of those that a mesh axis runs over, the one named last changes fastest.
Arguments:
- root_frame: float32 [2048, 1024], P(('pole', 'leaf')), parts along dimension 0, may hold values from -2 to 8, as said below
- top_lhat: float32 [3072, 256], P(('pole', 'leaf')), parts along dimension 0, may hold values from -0.21875 to 0.21875
- top_dinv: float32 [1024, 256], P(('pole', 'leaf')), parts along dimension 0, may hold values from -2 to 8, as said below
- mid_lhat: float32 [32, 768, 256], P(('pole', 'leaf')), parts along dimension 0, may hold values from -0.21875 to 0.21875
- mid_dinv: float32 [32, 256, 256], P(('pole', 'leaf')), parts along dimension 0, may hold values from -2 to 8, as said below
- leaf_lhat: float32 [64, 768, 256], P(('pole', 'leaf')), parts along dimension 0, may hold values from -0.21875 to 0.21875
- leaf_dinv: float32 [64, 256, 256], P(('pole', 'leaf')), parts along dimension 0, may hold values from -2 to 8, as said below
- top_columns: int32 [2], replicated, may hold values from 128 to 256
- mid_columns: int32 [16], replicated, may hold values from 128 to 256
- leaf_columns: int32 [32], replicated, may hold values from 128 to 256
- top_pattern: int32 [2, 3], replicated, may hold values from 0 to 3, as said below
- mid_parent: int32 [16], replicated, may hold values from 0 to 1, as said below
- leaf_parent: int32 [32], replicated, may hold values from 0 to 15, as said below
- mid_pattern: int32 [16, 3], replicated, may hold values from 0 to 3, as said below
- leaf_pattern: int32 [32, 3], replicated, may hold values from 0 to 3, as said below
- leaf_live: int32 [16], replicated, may hold values from 1 to 2, as said below
Outputs:
- top_diagonal: float32 [1024, 256], P(('pole', 'leaf')), parts along dimension 0
- top_coupling: float32 [3072, 256], P(('pole', 'leaf')), parts along dimension 0
- mid_diagonal: float32 [32, 256, 256], P(('pole', 'leaf')), parts along dimension 0
- mid_coupling: float32 [32, 768, 256], P(('pole', 'leaf')), parts along dimension 0
- leaf_diagonal: float32 [64, 256, 256], P(('pole', 'leaf')), parts along dimension 0
- leaf_coupling: float32 [64, 768, 256], P(('pole', 'leaf')), parts along dimension 0
There are 2 independent parts, one for each index of `pole`. A program takes and returns all parts, laid end to end along the dimension named above; an argument that names none is the same for every part. Nothing has to cross between parts.
Inputs may be any that keep to these rules, and one draw needn't show every extreme that they name: `root_frame`: Symmetric. `top_dinv`: each 256 x 256 block is symmetric. `mid_dinv`: each block is symmetric. `leaf_dinv`: each block is symmetric. `top_pattern`: each row holds 3 distinct increasing numbers of 0 to 3. mid_parent[j] is 2 * (j // 16) plus a number below 2: a level-1 supernode hangs under a level-2 supernode of its own group of 16 devices. leaf_parent[i] is one of the 4 level-1 supernodes numbered from 4 * (i // 8): a leaf hangs under a level-1 supernode of its own group of 4 devices. `mid_pattern`: each row starts with 0 (the parent) and goes on with 2 distinct increasing numbers of 1 to 3. `leaf_pattern`: each row starts with 0 (the parent) and goes on with 2 distinct increasing numbers of 1 to 3. The leaf supernodes of device d are its first leaf_live[d] slots; some device has all 2.
All inputs are finite; a program needn't handle non-finite values.
Results may differ from a plain program's by a relative error of at most 0.0003.
Values sent between devices are 32-bit elements; how exact they have to be, the bound alone decides.
A program may use at most 128 MiB of HBM per device.

v0:
```python
import jax
import jax.numpy as jnp
from jax import lax
from jax.sharding import PartitionSpec as P

SLOTS = 3
GROUP2 = 16
NODES2 = 2
GROUP1 = 4


highest = lax.Precision.HIGHEST


def from_partner(x, axis, apart):
    return lax.ppermute(x, axis, [(i, i ^ 1 << apart) for i in range(lax.axis_size(axis))])


def masked_inputs(lhat_block, dinv_block, used_width):
    block_size = lhat_block.shape[-1]
    column_keep = (jnp.arange(block_size, dtype=jnp.int32) < used_width).astype(lhat_block.dtype)
    lhat_masked = lhat_block * column_keep[None, :]
    dinv_masked = dinv_block * column_keep[:, None] * column_keep[None, :]
    return (lhat_masked, dinv_masked)


def solve_node(local_frame, lhat_block, dinv_block, used_width):
    lhat_masked, dinv_masked = masked_inputs(lhat_block, dinv_block, used_width)
    coupling = -jnp.dot(
        local_frame, lhat_masked, precision=highest, preferred_element_type=jnp.float32
    )
    diagonal = dinv_masked - jnp.dot(
        lhat_masked.T, coupling, precision=highest, preferred_element_type=jnp.float32
    )
    return (diagonal, coupling)


def extended_matrix(diagonal, coupling, local_frame):
    upper_row = jnp.concatenate([diagonal, coupling.T], axis=1)
    lower_row = jnp.concatenate([coupling, local_frame], axis=1)
    return jnp.concatenate([upper_row, lower_row], axis=0)


def select_frame(matrix, pattern, block_size):
    row_ids = (
        pattern[:, None] * block_size + jnp.arange(block_size, dtype=jnp.int32)[None, :]
    ).reshape(-1)
    picked = jnp.take(matrix, row_ids, axis=0)
    return jnp.take(picked, row_ids, axis=1)


def group_bits(members):
    bit_list = list(range(members.bit_length() - 1))
    return bit_list[::-1]


def collect(pieces, bit_list, swapper, position):
    gathered = pieces
    for bit_index in bit_list:
        received = swapper(gathered, bit_index)
        low_side = position >> bit_index & 1 == 0
        lower_part = jax.tree.map(
            lambda own_part, peer_part: jnp.where(low_side, own_part, peer_part), gathered, received
        )
        upper_part = jax.tree.map(
            lambda own_part, peer_part: jnp.where(low_side, peer_part, own_part), gathered, received
        )
        gathered = jax.tree.map(
            lambda first_part, second_part: jnp.stack([first_part, second_part]),
            lower_part,
            upper_part,
        )
    levels = len(bit_list)
    newest = list(reversed(bit_list))
    axis_order = sorted(range(levels), key=lambda axis_index: -newest[axis_index])

    def arrange(stacked, single):
        moved = jnp.transpose(stacked, tuple(axis_order) + tuple(range(levels, stacked.ndim)))
        return moved.reshape((2**levels,) + single.shape)

    return jax.tree.map(arrange, gathered, pieces)


def swap_factors(parts, bit_index):
    return from_partner(parts, "leaf", bit_index)


def swap_blocks(parts, bit_index):
    return from_partner((parts[0], parts[1]), "leaf", bit_index)


def swap_middle(parts, bit_index):
    return from_partner((parts[0], parts[1]), "leaf", bit_index)


def body(
    root_frame,
    top_lhat,
    top_dinv,
    mid_lhat,
    mid_dinv,
    leaf_lhat,
    leaf_dinv,
    top_columns,
    mid_columns,
    leaf_columns,
    top_pattern,
    mid_parent,
    leaf_parent,
    mid_pattern,
    leaf_pattern,
    leaf_live,
):
    device = lax.axis_index("leaf")
    block_size = top_dinv.shape[1]
    frame_size = SLOTS * block_size
    frame_rows = top_lhat.shape[0]
    diag_rows = top_dinv.shape[0]
    per_node = GROUP2 // NODES2
    member = device % GROUP2
    node_local = member // per_node
    row_block = member % per_node
    top_base = device // GROUP2 * NODES2
    own_top = top_base + node_local
    wide_bits = group_bits(GROUP2)
    root_whole = lax.all_gather(root_frame, "leaf", axis=0, tiled=True)
    group_patterns = lax.dynamic_slice_in_dim(top_pattern, top_base, NODES2, 0)
    frames_all = jax.vmap(lambda pattern: select_frame(root_whole, pattern, block_size))(
        group_patterns
    )
    lhat_all = collect(top_lhat, wide_bits, swap_factors, member)
    lhat_all = lhat_all.reshape(NODES2, frame_size, block_size)
    own_lhat = lax.dynamic_index_in_dim(lhat_all, node_local, 0, keepdims=False)
    own_frame = lax.dynamic_index_in_dim(frames_all, node_local, 0, keepdims=False)
    frame_part = lax.dynamic_slice_in_dim(own_frame, row_block * frame_rows, frame_rows, 0)
    used_width = top_columns[own_top]
    column_keep = (jnp.arange(block_size, dtype=jnp.int32) < used_width).astype(jnp.float32)
    lhat_whole = own_lhat * column_keep[None, :]
    lhat_rows = top_lhat * column_keep[None, :]
    coupling_rows = -jnp.dot(
        frame_part, lhat_whole, precision=highest, preferred_element_type=jnp.float32
    )
    partial_sum = jnp.dot(
        lhat_rows.T, coupling_rows, precision=highest, preferred_element_type=jnp.float32
    )
    for bit_index in group_bits(per_node):
        partial_sum = partial_sum + from_partner(partial_sum, "leaf", bit_index)
    row_ids = row_block * diag_rows + jnp.arange(diag_rows, dtype=jnp.int32)
    row_keep = (row_ids < used_width).astype(jnp.float32)
    dinv_rows = top_dinv * row_keep[:, None] * column_keep[None, :]
    diag_part = dinv_rows - lax.dynamic_slice_in_dim(
        partial_sum, row_block * diag_rows, diag_rows, 0
    )
    coupling_all, diagonal_all = collect((coupling_rows, diag_part), wide_bits, swap_blocks, member)
    coupling_all = coupling_all.reshape(NODES2, frame_size, block_size)
    diagonal_all = diagonal_all.reshape(NODES2, block_size, block_size)
    upper_mats = jax.vmap(extended_matrix)(diagonal_all, coupling_all, frames_all)
    own_parent = mid_parent[device] - top_base
    parent_matrix = lax.dynamic_index_in_dim(upper_mats, own_parent, 0, keepdims=False)
    mid_frame = select_frame(parent_matrix, mid_pattern[device], block_size)
    mid_diag, mid_coup = solve_node(mid_frame, mid_lhat[0], mid_dinv[0], mid_columns[device])
    mid_diagonal = mid_diag[None]
    mid_coupling = mid_coup[None]
    diag_group, coup_group = collect(
        (mid_diag, mid_coup), group_bits(GROUP1), swap_middle, device % GROUP1
    )
    mid_base = device // GROUP1 * GROUP1
    group_ids = mid_base + jnp.arange(GROUP1, dtype=jnp.int32)

    def middle_extended(diag_one, coup_one, node_index):
        above_matrix = lax.dynamic_index_in_dim(
            upper_mats, mid_parent[node_index] - top_base, 0, keepdims=False
        )
        above_frame = select_frame(above_matrix, mid_pattern[node_index], block_size)
        return extended_matrix(diag_one, coup_one, above_frame)

    lower_mats = jax.vmap(middle_extended)(diag_group, coup_group, group_ids)
    leaves = leaf_lhat.shape[0]

    def leaf_solve(lhat_one, dinv_one, node_index):
        parent = leaf_parent[node_index] - mid_base
        matrix = lax.dynamic_index_in_dim(lower_mats, parent, 0, keepdims=False)
        local_frame = select_frame(matrix, leaf_pattern[node_index], block_size)
        return solve_node(local_frame, lhat_one, dinv_one, leaf_columns[node_index])

    live_count = leaf_live[device]
    empty_diag = jnp.zeros((leaves, block_size, block_size), jnp.float32)
    empty_coup = jnp.zeros((leaves, frame_size, block_size), jnp.float32)
    base_index = device * leaves

    def slot_step(slot_index, current):
        diag_out, coup_out = current
        lhat_one = lax.dynamic_index_in_dim(leaf_lhat, slot_index, 0, keepdims=False)
        dinv_one = lax.dynamic_index_in_dim(leaf_dinv, slot_index, 0, keepdims=False)
        diag_one, coup_one = leaf_solve(lhat_one, dinv_one, base_index + slot_index)
        diag_out = lax.dynamic_update_index_in_dim(diag_out, diag_one, slot_index, 0)
        coup_out = lax.dynamic_update_index_in_dim(coup_out, coup_one, slot_index, 0)
        return (diag_out, coup_out)

    leaf_diagonal, leaf_coupling = lax.fori_loop(0, live_count, slot_step, (empty_diag, empty_coup))
    return (diag_part, coupling_rows, mid_diagonal, mid_coupling, leaf_diagonal, leaf_coupling)


def solution(mesh):
    in_specs = (
        P(("pole", "leaf"), None),
        P(("pole", "leaf"), None),
        P(("pole", "leaf"), None),
        P(("pole", "leaf"), None, None),
        P(("pole", "leaf"), None, None),
        P(("pole", "leaf"), None, None),
        P(("pole", "leaf"), None, None),
        P(),
        P(),
        P(),
        P(),
        P(),
        P(),
        P(),
        P(),
        P(),
    )
    out_specs = (
        P(("pole", "leaf"), None),
        P(("pole", "leaf"), None),
        P(("pole", "leaf"), None, None),
        P(("pole", "leaf"), None, None),
        P(("pole", "leaf"), None, None),
        P(("pole", "leaf"), None, None),
    )
    return jax.shard_map(body, mesh=mesh, in_specs=in_specs, out_specs=out_specs, check_vma=False)
```

profile of v0, /device:TPU:3, one launch (start us, length us, event | category | flops | bytes accessed | tf_op | source)
XLA Modules:
  0.0 480.8 jit_solution(7872795560996102290)
XLA Ops:
  7.9 2.4 collective-permute-start
  15.8 1.6 collective-permute-start.1
  18.1 3.1 collective-permute-done.1
  21.9 6.4 %collective-permute-done.2 = f32[2,2,96,256]{3,2,1,0:T(8,128)S(1)} collective-permute-done((f32[2,2,96,256]{3,2,1,0:T(8,128)S(1)}, f32[2,2,96,256]{3,2,1,0:T(8,128)S(1)}, u32[]{:S(2)}, u32[]{:S(2)}) %collective-permute-start.2) | collective-permute-done | bytes 393248 | tf_op jit(solution)/shard_map/ppermute | solution.py:16
  28.4 4.9 %collective-permute-start.3 = (f32[2,2,2,96,256]{4,3,2,1,0:T(8,128)S(1)}, f32[2,2,2,96,256]{4,3,2,1,0:T(8,128)S(1)}, u32[]{:S(2)}, u32[]{:S(2)}) collective-permute-start(f32[2,2,2,96,256]{4,3,2,1,0:T(8,128)S(1)} %pad_maximum_fusion.3), channel_id=1, source_target_pairs={{0,1},{1,0},{2,3},{3,2},{4,5},{5,4},{6,7},{7,6},{8,9},{9,8},{10,11... | collective-permute-start | bytes 2359304 | tf_op jit(solution)/shard_map/ppermute | solution.py:16
  33.6 1.7 collective-permute-done.3
  35.7 26.6 %all-gather.2.cloned.1.call-done = f32[1024,1024]{1,0:T(8,128)} async-done(((f32[64,1024]{1,0:T(8,128)}), f32[1024,1024]{1,0:T(8,128)}) %all-gather.2.cloned.1.call-update) | async-done | bytes 4194320 | tf_op jit(solution)/shard_map/all_gather | solution.py:126
  62.3 10.0 %gather_fusion.2 = f32[1536,1024]{1,0:T(8,128)} fusion(f32[1024,1024]{1,0:T(8,128)} %all-gather.2.cloned.1.call-done, s32[2048]{0:T(1024)S(1)} %pad_clamp_fusion.1), kind=kCustom, calls=%fused_computation.2 | custom fusion | bytes 12589056 | tf_op jit(solution)/shard_map/vmap(jit(_take))/gather | solution.py:48
  72.3 6.7 %copy.36 = f32[2,768,1024]{1,2,0:T(8,128)} copy(f32[2,768,1024]{2,1,0:T(8,128)} %bitcast.209) | data formatting | bytes 12582912 | tf_op jit(solution)/shard_map/vmap(jit(_take))/gather | solution.py:48
  78.9 5.9 %broadcast_select_fusion.2 = f32[2,768,1024]{1,2,0:T(8,128)} fusion(f32[2,768,1024]{1,2,0:T(8,128)} %copy.36, pred[2,768]{1,0:T(4,128)(4,1)S(1)} %compare_and_fusion.2), kind=kLoop, calls=%fused_computation.49 | loop fusion | flops 1572864 | bytes 12584448 | tf_op jit(solution)/shard_map/vmap(jit(_take))/select_n | solution.py:48
  84.9 28.4 %gather_fusion.7 = f32[1536,768]{1,0:T(8,128)} fusion(f32[2,768,1024]{1,2,0:T(8,128)} %broadcast_select_fusion.2, s32[1536]{0:T(1024)S(1)} %reshape.398), kind=kCustom, calls=%fused_computation.7 | custom fusion | bytes 9449472 | tf_op jit(solution)/shard_map/vmap(jit(_take))/gather | solution.py:49
  113.3 6.1 %copy.37 = f32[2,768,768]{1,2,0:T(8,128)} copy(f32[2,768,768]{2,1,0:T(8,128)} %bitcast.210) | data formatting | bytes 9437184 | tf_op jit(solution)/shard_map/vmap(jit(_take))/gather | solution.py:49
  119.4 2.7 broadcast_select_fusion.3
  123.1 1.7 collective-permute-start.11
  127.0 2.9 collective-permute-done.11
  129.9 4.0 collective-permute-done.4
  135.8 5.1 %collective-permute-done.5 = f32[256,256]{1,0:T(8,128)S(1)} collective-permute-done((f32[256,256]{1,0:T(8,128)S(1)}, f32[256,256]{1,0:T(8,128)S(1)}, u32[]{:S(2)}, u32[]{:S(2)}) %collective-permute-start.5) | collective-permute-done | bytes 262176 | tf_op jit(solution)/shard_map/ppermute | solution.py:16
  140.9 1.9 collective-permute-start.6
  149.5 4.1 collective-permute-done.13
  156.3 1.7 collective-permute-done.9
  158.1 1.8 collective-permute-start.10
  159.9 2.5 fusion.49
  164.2 1.5 pad_maximum_fusion.1
  165.8 2.9 copy.43
  168.7 3.5 maximum_maximum_fusion.1
  172.2 3.3 copy-done.1
  175.5 2.6 dynamic-slice_bitcast_fusion.1
  178.1 6.1 %gather_fusion.3 = f32[768,1024]{1,0:T(8,128)S(1)} fusion(f32[1024,1024]{1,0:T(8,128)} %dynamic-slice_bitcast_fusion.1, s32[1024]{0:T(1024)S(1)} %pad_clamp_fusion.3), kind=kCustom, calls=%fused_computation.3 | custom fusion | bytes 6294528 | tf_op jit(solution)/shard_map/jit(_take)/gather | solution.py:48
  184.2 1.9 broadcast_select_fusion.4
  186.1 2.4 copy.44
  188.5 3.5 gather_fusion.4
  192.0 5.8 %fusion.21 = f32[768,256]{1,0:T(8,128)S(1)} fusion(f32[768,768]{1,0:T(8,128)} %gather_fusion.4, pred[768]{0:T(1024)(128)(4,1)S(1)} %compare_and_fusion.3, f32[1,768,256]{2,1,0:T(8,128)} %param.21, f32[256]{0:T(256)S(1)} %compare_convert_fusion.1), kind=kOutput, calls=%fused_computation.60 | convolution fusion | flops 1812922368 | bytes 3933952 | tf_op jit(solution)/shard_map/dot_general | solution.py:29
  199.1 19.3 %while.14 = (s32[]{:T(128)}, f32[2,1024,1024]{2,1,0:T(8,128)}, s32[4,3]{1,0:T(4,128)S(1)}, f32[4,1,1024,1024]{3,2,1,0:T(8,128)}, s32[]{:T(128)}) while((s32[]{:T(128)}, f32[2,1024,1024]{2,1,0:T(8,128)}, s32[4,3]{1,0:T(4,128)S(1)}, f32[4,1,1024,1024]{3,2,1,0:T(8,128)}, s32[]{:T(128)}) %tuple.71), condition=%wide.while_cond, body=%wide.while_body.sunk | while | flops 2 | bytes 8388713 | solution.py:171
  199.1 4.8 bitcast_dynamic-update-slice_fusion.5
  203.9 4.8 %bitcast_dynamic-update-slice_fusion.5 = f32[4,1,1024,1024]{3,2,1,0:T(8,128)} fusion(f32[4,1,1024,1024]{3,2,1,0:T(8,128)} %get-tuple-element.311, s32[]{:T(128)S(6)} %copy.69, f32[2,1024,1024]{2,1,0:T(8,128)} %get-tuple-element.314, s32[]{:T(128)S(1)} %bitcast.222), kind=kLoop, calls=%fused_computation.10.clone.1 | loop fusion | bytes 8388616 | tf_op jit(solution)/shard_map/vmap(jit(dynamic_index_in_dim))/gather
  208.7 4.9 %bitcast_dynamic-update-slice_fusion.5 = f32[4,1,1024,1024]{3,2,1,0:T(8,128)} fusion(f32[4,1,1024,1024]{3,2,1,0:T(8,128)} %get-tuple-element.311, s32[]{:T(128)S(6)} %copy.69, f32[2,1024,1024]{2,1,0:T(8,128)} %get-tuple-element.314, s32[]{:T(128)S(1)} %bitcast.222), kind=kLoop, calls=%fused_computation.10.clone.1 | loop fusion | bytes 8388616 | tf_op jit(solution)/shard_map/vmap(jit(dynamic_index_in_dim))/gather
  213.6 4.8 bitcast_dynamic-update-slice_fusion.5
  218.4 60.2 %gather_fusion.8 = f32[3072,1024]{1,0:T(8,128)} fusion(f32[4,1024,1024]{2,1,0:T(8,128)} %bitcast.204, s32[3072]{0:T(1024)S(1)} %reshape.404), kind=kCustom, calls=%fused_computation.8 | custom fusion | bytes 25190400 | tf_op jit(solution)/shard_map/vmap(jit(_take))/gather | solution.py:48
  278.6 12.8 %copy.51 = f32[4,768,1024]{1,2,0:T(8,128)} copy(f32[4,768,1024]{2,1,0:T(8,128)} %bitcast.205) | data formatting | bytes 25165824 | tf_op jit(solution)/shard_map/vmap(jit(_take))/gather | solution.py:48
  291.3 1.4 convolution_subtract_fusion.1
  296.2 10.4 %broadcast_select_fusion.1 = f32[4,768,1024]{1,2,0:T(8,128)} fusion(f32[4,768,1024]{1,2,0:T(8,128)} %copy.51, pred[4,768]{1,0:T(4,128)(4,1)S(1)} %compare_and_fusion.1), kind=kLoop, calls=%fused_computation.45 | loop fusion | flops 3145728 | bytes 25168896 | tf_op jit(solution)/shard_map/vmap(jit(_take))/select_n | solution.py:48
  307.4 56.3 %gather_fusion.9 = f32[3072,768]{1,0:T(8,128)} fusion(f32[4,768,1024]{1,2,0:T(8,128)} %broadcast_select_fusion.1, s32[3072]{0:T(1024)S(1)} %reshape.404), kind=kCustom, calls=%fused_computation.9 | custom fusion | bytes 18898944 | tf_op jit(solution)/shard_map/vmap(jit(_take))/gather | solution.py:49
  363.7 9.6 %copy.52 = f32[4,768,768]{1,2,0:T(8,128)} copy(f32[4,768,768]{2,1,0:T(8,128)} %bitcast.206) | data formatting | bytes 18874368 | tf_op jit(solution)/shard_map/vmap(jit(_take))/gather | solution.py:49
  373.4 8.2 %select_bitcast_fusion = f32[4,768,768]{2,1,0:T(8,128)} fusion(f32[4,768,768]{1,2,0:T(8,128)} %copy.52, pred[4,768]{1,0:T(4,128)(4,1)S(1)} %compare_and_fusion.1), kind=kLoop, calls=%fused_computation.43 | loop fusion | flops 2359296 | bytes 18877440 | tf_op jit(solution)/shard_map/vmap(jit(_take))/select_n | solution.py:49
  383.1 2.6 copy.47
  385.7 1.7 select_bitcast_fusion.2
  388.8 2.3 pad_maximum_fusion
  391.1 5.4 %copy.53 = f32[4,256,1024]{2,1,0:T(8,128)} copy(f32[4,256,1024]{1,2,0:T(8,128)} %pad_maximum_fusion) | data formatting | bytes 8388608 | tf_op jit(solution)/shard_map/vmap()/concatenate | solution.py:39
  396.5 11.0 %maximum_maximum_fusion = f32[4,1024,1024]{2,1,0:T(8,128)} fusion(f32[4,768,768]{2,1,0:T(8,128)} %select_bitcast_fusion, f32[4,768,256]{2,1,0:T(8,128)S(1)} %bitcast.208, f32[4,256,1024]{2,1,0:T(8,128)} %copy.53), kind=kLoop, calls=%fused_computation.42 | loop fusion | flops 8388608 | bytes 33554432 | tf_op jit(solution)/shard_map/vmap()/concatenate | solution.py:41
  409.6 64.3 %while.13 = (s32[]{:T(128)}, f32[2,256,256]{2,1,0:T(8,128)}, f32[2,768,256]{2,1,0:T(8,128)}, s32[]{:T(128)}, f32[2,256,256]{2,1,0:T(8,128)}, /*index=5*/s32[]{:T...) while((s32[]{:T(128)}, f32[2,256,256]{2,1,0:T(8,128)}, ...), condition=%wide.region_1.2_spmd, body=%wide.region_0.1_spmd.sunk | while | flops 2418091008 | bytes 51431132 | solution.py:200
  412.9 4.8 dynamic-slice_bitcast_fusion.3
  418.4 6.1 %gather_fusion = f32[768,1024]{1,0:T(8,128)S(1)} fusion(f32[1024,1024]{1,0:T(8,128)} %dynamic-slice_bitcast_fusion.3, s32[1024]{0:T(1024)S(1)} %pad_clamp_fusion.5), kind=kCustom, calls=%fused_computation.clone.1 | custom fusion | bytes 6294528 | tf_op jit(solution)/shard_map/while/body/jit(_take)/gather | solution.py:48
  424.6 1.9 broadcast_select_fusion.6
  426.5 2.4 copy.63
  428.9 3.5 gather_fusion.1
  432.4 6.8 %bitcast_dynamic-update-slice_fusion.4 = (f32[2,768,256]{2,1,0:T(8,128)}, f32[768,256]{1,0:T(8,128)S(1)}) fusion(f32[2,768,256]{2,1,0:T(8,128)} %get-tuple-element.337, s32[]{:T(128)S(6)} %select_n.578, f32[2,768,256]{2,1,0:T(8,128)} %get-tuple-element.359, f32[256]{0:T(256)S(1)} %compare_convert_fusion.5, f32[768,768]{1,0:T(8,128)} %gather_fusion.1, ...), kind=kOutput, calls=%fused_computation.22.clone.1 | convolution fusion | flops 1812922368 | bytes 4721408 | tf_op jit(solution)/shard_map/while/body/dot_general | solution.py:29
  439.3 1.4 fusion.57
  444.8 4.8 dynamic-slice_bitcast_fusion.3
  450.3 6.1 %gather_fusion = f32[768,1024]{1,0:T(8,128)S(1)} fusion(f32[1024,1024]{1,0:T(8,128)} %dynamic-slice_bitcast_fusion.3, s32[1024]{0:T(1024)S(1)} %pad_clamp_fusion.5), kind=kCustom, calls=%fused_computation.clone.1 | custom fusion | bytes 6294528 | tf_op jit(solution)/shard_map/while/body/jit(_take)/gather | solution.py:48
  456.5 1.9 broadcast_select_fusion.6
  458.4 2.4 copy.63
  460.8 3.5 gather_fusion.1
  464.3 6.8 %bitcast_dynamic-update-slice_fusion.4 = (f32[2,768,256]{2,1,0:T(8,128)}, f32[768,256]{1,0:T(8,128)S(1)}) fusion(f32[2,768,256]{2,1,0:T(8,128)} %get-tuple-element.337, s32[]{:T(128)S(6)} %select_n.578, f32[2,768,256]{2,1,0:T(8,128)} %get-tuple-element.359, f32[256]{0:T(256)S(1)} %compare_convert_fusion.5, f32[768,768]{1,0:T(8,128)} %gather_fusion.1, ...), kind=kOutput, calls=%fused_computation.22.clone.1 | convolution fusion | flops 1812922368 | bytes 4721408 | tf_op jit(solution)/shard_map/while/body/dot_general | solution.py:29
  471.2 1.4 fusion.57
  (186 shorter events, 41.7 us)
Async XLA Ops:
  7.2 55.1 %all-gather.2.cloned.1.call-start = ((), (), s32[]{:S(2)}) async-start(), calls=%async_computation | async-start | bytes 4456448 | tf_op jit(solution)/shard_map/all_gather | solution.py:126
  7.9 7.0 %collective-permute-start = (f32[96,256]{1,0:T(8,128)}, f32[96,256]{1,0:T(8,128)S(1)}, u32[]{:S(2)}, u32[]{:S(2)}) collective-permute-start(f32[96,256]{1,0:T(8,128)} %param.19), channel_id=1, source_target_pairs={{0,8},{1,9},{2,10},{3,11},{4,12},{5,13},{6,14},{7,15},{8,0},{9,1},... | collective-permute-start | bytes 294920 | tf_op jit(solution)/shard_map/ppermute | solution.py:16
  15.8 5.3 %collective-permute-start.1 = (f32[2,96,256]{2,1,0:T(8,128)S(1)}, f32[2,96,256]{2,1,0:T(8,128)S(1)}, u32[]{:S(2)}, u32[]{:S(2)}) collective-permute-start(f32[2,96,256]{2,1,0:T(8,128)S(1)} %pad_maximum_fusion.9), channel_id=1, source_target_pairs={{0,4},{1,5},{2,6},{3,7},{4,0},{5,1},{6,2},{7,3},{8,12},{9,13},{10,... | collective-permute-start | bytes 589832 | tf_op jit(solution)/shard_map/ppermute | solution.py:16
  21.2 7.1 %collective-permute-start.2 = (f32[2,2,96,256]{3,2,1,0:T(8,128)S(1)}, f32[2,2,96,256]{3,2,1,0:T(8,128)S(1)}, u32[]{:S(2)}, u32[]{:S(2)}) collective-permute-start(f32[2,2,96,256]{3,2,1,0:T(8,128)S(1)} %pad_maximum_fusion.6), channel_id=1, source_target_pairs={{0,2},{1,3},{2,0},{3,1},{4,6},{5,7},{6,4},{7,5},{8,10},{9,11},{10,... | collective-permute-start | bytes 1179656 | tf_op jit(solution)/shard_map/ppermute | solution.py:16
  28.4 6.8 %collective-permute-start.3 = (f32[2,2,2,96,256]{4,3,2,1,0:T(8,128)S(1)}, f32[2,2,2,96,256]{4,3,2,1,0:T(8,128)S(1)}, u32[]{:S(2)}, u32[]{:S(2)}) collective-permute-start(f32[2,2,2,96,256]{4,3,2,1,0:T(8,128)S(1)} %pad_maximum_fusion.3), channel_id=1, source_target_pairs={{0,1},{1,0},{2,3},{3,2},{4,5},{5,4},{6,7},{7,6},{8,9},{9,8},{10,11... | collective-permute-start | bytes 2359304 | tf_op jit(solution)/shard_map/ppermute | solution.py:16
  119.4 3.3 copy-start.11
  119.4 6.4 %copy-start.16 = (s32[16]{0:T(128)S(1)}, s32[16]{0:T(128)}, u32[]{:S(2)}) copy-start(s32[16]{0:T(128)} %param.26) | copy-start | bytes 196
  119.4 7.0 %copy-start = (s32[16]{0:T(128)S(1)}, s32[16]{0:T(128)}, u32[]{:S(2)}) copy-start(s32[16]{0:T(128)} %param.29) | copy-start | bytes 196
  122.0 22.1 %copy-start.14 = (f32[32,256]{1,0:T(8,128)S(1)}, f32[32,256]{1,0:T(8,128)}, u32[]{:S(2)}) copy-start(f32[32,256]{1,0:T(8,128)} %param.20) | copy-start | bytes 98308
  122.1 25.3 %copy-start.12 = (f32[1,256,256]{2,1,0:T(8,128)S(1)}, f32[1,256,256]{2,1,0:T(8,128)}, u32[]{:S(2)}) copy-start(f32[1,256,256]{2,1,0:T(8,128)} %param.22) | copy-start | bytes 786436
  122.1 25.4 %copy-start.17 = (s32[16]{0:T(128)S(1)}, s32[16]{0:T(128)}, u32[]{:S(2)}) copy-start(s32[16]{0:T(128)} %param.33) | copy-start | bytes 196
  122.1 26.0 %copy-start.15 = (s32[32,3]{0,1:T(4,128)S(1)}, s32[32,3]{0,1:T(4,128)}, u32[]{:S(2)}) copy-start(s32[32,3]{0,1:T(4,128)} %param.32) | copy-start | bytes 1156
  122.7 31.0 %copy-start.8 = (f32[96,256]{1,0:T(8,128)}, f32[96,256]{1,0:T(8,128)S(1)}, u32[]{:S(2)}) copy-start(f32[96,256]{1,0:T(8,128)S(1)} %convolution_negate_fusion) | copy-start | bytes 294916
  123.1 6.7 %collective-permute-start.11 = (f32[96,256]{1,0:T(8,128)S(1)}, f32[96,256]{1,0:T(8,128)S(1)}, u32[]{:S(2)}, u32[]{:S(2)}) collective-permute-start(f32[96,256]{1,0:T(8,128)S(1)} %convolution_negate_fusion), channel_id=1, source_target_pairs={{0,8},{1,9},{2,10},{3,11},{4,12},{5,13},{6,14},{7,15},{8,0},{9,1},... | collective-permute-start | bytes 294920 | tf_op jit(solution)/shard_map/ppermute | solution.py:16
  124.8 9.1 %collective-permute-start.4 = (f32[256,256]{1,0:T(8,128)S(1)}, f32[256,256]{1,0:T(8,128)S(1)}, u32[]{:S(2)}, u32[]{:S(2)}) collective-permute-start(f32[256,256]{1,0:T(8,128)S(1)} %fusion.35), channel_id=1, source_target_pairs={{0,4},{1,5},{2,6},{3,7},{4,0},{5,1},{6,2},{7,3},{8,12},{9,13},{10,... | collective-permute-start | bytes 786440 | tf_op jit(solution)/shard_map/ppermute | solution.py:16
  134.0 6.9 %collective-permute-start.5 = (f32[256,256]{1,0:T(8,128)S(1)}, f32[256,256]{1,0:T(8,128)S(1)}, u32[]{:S(2)}, u32[]{:S(2)}) collective-permute-start(f32[256,256]{1,0:T(8,128)S(1)} %add.390), channel_id=1, source_target_pairs={{0,2},{1,3},{2,0},{3,1},{4,6},{5,7},{6,4},{7,5},{8,10},{9,11},{10,... | collective-permute-start | bytes 786440 | tf_op jit(solution)/shard_map/ppermute | solution.py:16
  135.2 7.6 %collective-permute-start.12 = (f32[2,96,256]{2,1,0:T(8,128)S(1)}, f32[2,96,256]{2,1,0:T(8,128)S(1)}, u32[]{:S(2)}, u32[]{:S(2)}) collective-permute-start(f32[2,96,256]{2,1,0:T(8,128)S(1)} %pad_maximum_fusion.10), channel_id=1, source_target_pairs={{0,4},{1,5},{2,6},{3,7},{4,0},{5,1},{6,2},{7,3},{8,12},{9,13},{10,... | collective-permute-start | bytes 589832 | tf_op jit(solution)/shard_map/ppermute | solution.py:16
  140.9 3.2 collective-permute-start.6
  142.9 10.7 %collective-permute-start.13 = (f32[2,2,96,256]{3,2,1,0:T(8,128)S(1)}, f32[2,2,96,256]{3,2,1,0:T(8,128)S(1)}, u32[]{:S(2)}, u32[]{:S(2)}) collective-permute-start(f32[2,2,96,256]{3,2,1,0:T(8,128)S(1)} %pad_maximum_fusion.7), channel_id=1, source_target_pairs={{0,2},{1,3},{2,0},{3,1},{4,6},{5,7},{6,4},{7,5},{8,10},{9,11},{10,... | collective-permute-start | bytes 1179656 | tf_op jit(solution)/shard_map/ppermute | solution.py:16
  144.2 9.5 %copy-start.13 = (f32[32,256]{1,0:T(8,128)}, f32[32,256]{1,0:T(8,128)S(1)}, u32[]{:S(2)}) copy-start(f32[32,256]{1,0:T(8,128)S(1)} %fusion.38) | copy-start | bytes 98308
  144.3 4.7 collective-permute-start.7
  148.9 11.0 %copy-start.2 = (f32[2,768,768]{1,2,0:T(8,128)S(1)}, f32[2,768,768]{1,2,0:T(8,128)}, u32[]{:S(2)}) copy-start(f32[2,768,768]{1,2,0:T(8,128)} %copy.37) | copy-start | bytes 14155780
  148.9 4.8 collective-permute-start.8
  153.8 4.2 collective-permute-start.9
  155.1 7.6 %collective-permute-start.14 = (f32[2,2,2,96,256]{4,3,2,1,0:T(8,128)S(1)}, f32[2,2,2,96,256]{4,3,2,1,0:T(8,128)}, u32[]{:S(2)}, u32[]{:S(2)}) collective-permute-start(f32[2,2,2,96,256]{4,3,2,1,0:T(8,128)S(1)} %pad_maximum_fusion.4), channel_id=1, source_target_pairs={{0,1},{1,0},{2,3},{3,2},{4,5},{5,4},{6,7},{7,6},{8,9},{9,8},{10,11... | collective-permute-start | bytes 2359304 | tf_op jit(solution)/shard_map/ppermute | solution.py:16
  158.1 4.3 collective-permute-start.10
  172.2 3.3 copy-start.1
  197.8 95.3 %copy-start.4 = (f32[768,256]{1,0:T(8,128)}, f32[768,256]{1,0:T(8,128)S(1)}, u32[]{:S(2)}) copy-start(f32[768,256]{1,0:T(8,128)S(1)} %fusion.21) | copy-start | bytes 2359300
  197.8 95.3 %collective-permute-start.17 = (f32[768,256]{1,0:T(8,128)S(1)}, f32[768,256]{1,0:T(8,128)}, u32[]{:S(2)}, u32[]{:S(2)}) collective-permute-start(f32[768,256]{1,0:T(8,128)S(1)} %fusion.21), channel_id=1, source_target_pairs={{0,2},{1,3},{2,0},{3,1},{4,6},{5,7},{6,4},{7,5},{8,10},{9,11},{10,... | collective-permute-start | bytes 2359304 | tf_op jit(solution)/shard_map/ppermute | solution.py:16
  278.6 12.8 %copy-start.7 = (f32[1,768,256]{2,1,0:T(8,128)S(1)}, f32[1,768,256]{2,1,0:T(8,128)}, u32[]{:S(2)}) copy-start(f32[1,768,256]{2,1,0:T(8,128)} %param.21) | copy-start | bytes 2359300
  292.8 80.5 %collective-permute-start.15 = (f32[256,256]{0,1:T(8,128)S(1)}, f32[256,256]{0,1:T(8,128)S(1)}, u32[]{:S(2)}, u32[]{:S(2)}) collective-permute-start(f32[256,256]{0,1:T(8,128)S(1)} %convolution_subtract_fusion.1), channel_id=1, source_target_pairs={{0,2},{1,3},{2,0},{3,1},{4,6},{5,7},{6,4},{7,5},{8,10},{9,11},{10,... | collective-permute-start | bytes 786440 | tf_op jit(solution)/shard_map/ppermute | solution.py:16
  295.6 90.1 %collective-permute-start.18 = (f32[2,768,256]{2,1,0:T(8,128)}, f32[2,768,256]{2,1,0:T(8,128)}, u32[]{:S(2)}, u32[]{:S(2)}) collective-permute-start(f32[2,768,256]{2,1,0:T(8,128)} %pad_maximum_fusion.2), channel_id=1, source_target_pairs={{0,1},{1,0},{2,3},{3,2},{4,5},{5,4},{6,7},{7,6},{8,9},{9,8},{10,11... | collective-permute-start | bytes 4718600 | tf_op jit(solution)/shard_map/ppermute | solution.py:16
  373.4 8.3 %collective-permute-start.16 = (f32[2,256,256]{1,2,0:T(8,128)S(1)}, f32[2,256,256]{1,2,0:T(8,128)S(1)}, u32[]{:S(2)}, u32[]{:S(2)}) collective-permute-start(f32[2,256,256]{1,2,0:T(8,128)S(1)} %pad_maximum_fusion.5), channel_id=1, source_target_pairs={{0,1},{1,0},{2,3},{3,2},{4,5},{5,4},{6,7},{7,6},{8,9},{9,8},{10,11... | collective-permute-start | bytes 1572872 | tf_op jit(solution)/shard_map/ppermute | solution.py:16
  387.6 1.2 copy-start.5
  396.5 13.1 %copy-start.18 = (s32[32]{0:T(128)S(1)}, s32[32]{0:T(128)}, u32[]{:S(2)}) copy-start(s32[32]{0:T(128)} %param.27) | copy-start | bytes 388
  396.5 13.1 %copy-start.19 = (s32[32]{0:T(128)S(1)}, s32[32]{0:T(128)}, u32[]{:S(2)}) copy-start(s32[32]{0:T(128)} %param.30) | copy-start | bytes 388
  432.4 6.9 %copy-start.3 = (f32[2,768,256]{2,1,0:T(8,128)S(1)}, f32[2,768,256]{2,1,0:T(8,128)}, u32[]{:S(2)}) copy-start(f32[2,768,256]{2,1,0:T(8,128)} %get-tuple-element.359) | copy-start | bytes 4718596 | tf_op jit(solution)/shard_map/while
  432.4 6.9 %copy-start.6 = (f32[2,256,256]{2,1,0:T(8,128)S(1)}, f32[2,256,256]{2,1,0:T(8,128)}, u32[]{:S(2)}) copy-start(f32[2,256,256]{2,1,0:T(8,128)} %get-tuple-element.356) | copy-start | bytes 1572868 | tf_op jit(solution)/shard_map/while
  432.4 6.9 %copy-start.9 = (f32[2,256,256]{2,1,0:T(8,128)S(1)}, f32[2,256,256]{2,1,0:T(8,128)}, u32[]{:S(2)}) copy-start(f32[2,256,256]{2,1,0:T(8,128)} %get-tuple-element.336) | copy-start | bytes 1572868 | tf_op jit(solution)/shard_map/while
  440.7 0.8 copy-start.10
  464.3 6.9 %copy-start.3 = (f32[2,768,256]{2,1,0:T(8,128)S(1)}, f32[2,768,256]{2,1,0:T(8,128)}, u32[]{:S(2)}) copy-start(f32[2,768,256]{2,1,0:T(8,128)} %get-tuple-element.359) | copy-start | bytes 4718596 | tf_op jit(solution)/shard_map/while
  464.3 6.9 %copy-start.6 = (f32[2,256,256]{2,1,0:T(8,128)S(1)}, f32[2,256,256]{2,1,0:T(8,128)}, u32[]{:S(2)}) copy-start(f32[2,256,256]{2,1,0:T(8,128)} %get-tuple-element.356) | copy-start | bytes 1572868 | tf_op jit(solution)/shard_map/while
  464.3 6.9 %copy-start.9 = (f32[2,256,256]{2,1,0:T(8,128)S(1)}, f32[2,256,256]{2,1,0:T(8,128)}, u32[]{:S(2)}) copy-start(f32[2,256,256]{2,1,0:T(8,128)} %get-tuple-element.336) | copy-start | bytes 1572868 | tf_op jit(solution)/shard_map/while
  472.6 0.8 copy-start.10
Sparse Core Ops, SparseCore 0:
  10.1 52.0 all-gather.1
where the time goes:
time: 485 us; the launch traced here: 481 us
  local copies, waits for them, and re-layouts  288 us (59%)
  other arithmetic  68.2 us (14%)
  waiting for transfers between devices  56.3 us (12%)
  starting transfers between devices  24.8 us (5%)
  matrix products  24.8 us (5%)
  between operations  15.4 us (3%)
    gather x8, local copies, waits for them, and re-layouts, select_frame(): return jnp.take(picked, row_ids, axis=1)  111 us
    gather x8, local copies, waits for them, and re-layouts, select_frame(): picked = jnp.take(matrix, row_ids, axis=0)  108 us
    ppermute x19, waiting for transfers between devices, from_partner(): lax.ppermute(x, axis, [(i, i ^ 1 << apart) for i in range(lax.axis_size(a...  29 us
    all_gather x1, waiting for transfers between devices, body(): root_whole = lax.all_gather(root_frame, 'leaf', axis=0, tiled=True)  26.6 us
    ppermute x19, starting transfers between devices, from_partner(): lax.ppermute(x, axis, [(i, i ^ 1 << apart) for i in range(lax.axis_size(a...  24.7 us
    select_n x5, other arithmetic, select_frame(): picked = jnp.take(matrix, row_ids, axis=0)  22 us
    dot_general x3, matrix products, solve_node(): jnp.dot(local_frame, lhat_masked, precision=highest, preferred_element_ty...  19.5 us
    gather x8, local copies, waits for them, and re-layouts  19.3 us
  transfers between devices with their start and end apart: 20, of which 9 were waited for; matrix products, arithmetic and copies ran while one was open for 42% of the time, Pallas kernels for 0%

commit v1 on v0

v1 whole, which is shorter than its diff:
```python
import functools

import jax
import jax.numpy as jnp
from jax import lax
from jax.experimental import pallas as pl
from jax.experimental.pallas import tpu as pltpu
from jax.sharding import PartitionSpec as P

SLOTS = 3
GROUP2 = 16
NODES2 = 2
GROUP1 = 4

MESH = pl.DeviceIdType.MESH
f32 = jnp.float32
bf16 = jnp.bfloat16


def split(value):
    high = value.astype(bf16)
    low = (value - high.astype(f32)).astype(bf16)
    return high, low


def remote(src, dst, send_sem, recv_sem, target):
    return pltpu.make_async_remote_copy(
        src_ref=src,
        dst_ref=dst,
        send_sem=send_sem,
        recv_sem=recv_sem,
        device_id={"leaf": target},
        device_id_type=MESH,
    )


class Spread:
    def __init__(self, own, whole, group, sems, me):
        self.own, self.whole, self.group = own, whole, group
        self.rows = own.shape[0]
        self.recv, self.up, self.down, self.side, self.core, self.local = sems
        self.base = me - lax.rem(me, group)

    def block(self, device):
        start = (device - self.base) * self.rows
        return self.whole.at[pl.ds(pl.multiple_of(start, 8), self.rows)]

    def copy(self, device, target, sems, own=False):
        slot = device - self.base
        return remote(
            self.own if own else self.block(device),
            self.block(device),
            sems.at[slot],
            self.recv.at[slot],
            target,
        )

    def keep(self, me):
        return pltpu.make_async_copy(self.own, self.block(me), self.local.at[0])

    def arrived(self, device, me):
        self.copy(device, me, self.core).wait_recv()


def gather_kernel(
    n,
    root_in,
    tl_in,
    td_in,
    ml_in,
    md_in,
    root_all,
    tl_all,
    td_all,
    ml_all,
    md_all,
    *sems,
):
    me = lax.axis_index("leaf")
    core = lax.rem(me, 2)
    side = lax.rem(me // 2, 2)
    cpeer = me + 1 - 2 * core
    xpeer = me + 2 - 4 * side
    root = Spread(root_in, root_all, n, sems[0:6], me)
    tl = Spread(tl_in, tl_all, GROUP2, sems[6:12], me)
    td = Spread(td_in, td_all, GROUP2, sems[12:18], me)
    ml = Spread(ml_in, ml_all, GROUP1, sems[18:24], me)
    md = Spread(md_in, md_all, GROUP1, sems[24:30], me)
    tops = (tl, td)
    mids = (ml, md)

    line = n // GROUP1
    place = me // GROUP1
    top_line = GROUP2 // GROUP1
    top_place = lax.rem(me, GROUP2) // GROUP1
    has_up = place < line - 1
    has_down = place > 0

    barrier = pltpu.get_barrier_semaphore()
    for peer in (cpeer, xpeer):
        pl.semaphore_signal(barrier, inc=1, device_id={"leaf": peer}, device_id_type=MESH)

    @pl.when(has_up)
    def _():
        pl.semaphore_signal(barrier, inc=1, device_id={"leaf": me + GROUP1}, device_id_type=MESH)

    @pl.when(has_down)
    def _():
        pl.semaphore_signal(barrier, inc=1, device_id={"leaf": me - GROUP1}, device_id_type=MESH)

    for part in (root,) + tops + mids:
        part.keep(me).start()
    peers = 2 + jnp.minimum(place, 1) + jnp.minimum(line - 1 - place, 1)
    pl.semaphore_wait(barrier, peers)

    def along(part, device, go_up, ok, act, own=False):
        if go_up:
            @pl.when(ok)
            def _():
                act(part.copy(device, me + GROUP1, part.up, own))
        else:
            @pl.when(ok)
            def _():
                act(part.copy(device, me - GROUP1, part.down, own))

    def start(copy):
        copy.start()

    def wait_send(copy):
        copy.wait_send()

    top_up = top_place < top_line - 1
    top_down = top_place > 0

    def own_copies(act):
        act(root.copy(me, xpeer, root.side, True))
        for part in tops:
            along(part, me, True, top_up, act, True)
            along(part, me, False, top_down, act, True)
        along(root, me, True, has_up, act, True)
        along(root, me, False, has_down, act, True)
        for part in tops:
            act(part.copy(me, xpeer, part.side, True))
        for part in (root,) + tops:
            act(part.copy(me, cpeer, part.core, True))
        for part in mids:
            act(part.copy(me, xpeer, part.side, True))
            act(part.copy(me, cpeer, part.core, True))

    own_copies(start)

    root.arrived(xpeer, me)
    along(root, xpeer, True, has_up, start)
    along(root, xpeer, False, has_down, start)
    root.copy(xpeer, cpeer, root.core).start()

    def step(s, carry):
        for go_up in (True, False):
            shift = -s * GROUP1 if go_up else s * GROUP1
            got_top = (top_place >= s) if go_up else (top_place + s < top_line)
            got_root = (place >= s) if go_up else (place + s < line)

            @pl.when(got_top)
            def _():
                for part in tops:
                    part.arrived(me + shift, me)
                    along(part, me + shift, go_up, top_up if go_up else top_down, start)
                    part.copy(me + shift, xpeer, part.side).start()
                    part.copy(me + shift, cpeer, part.core).start()

            @pl.when(got_root)
            def _():
                for device in (me, xpeer):
                    root.arrived(device + shift, me)
                    along(root, device + shift, go_up, has_up if go_up else has_down, start)
                    root.copy(device + shift, cpeer, root.core).start()

        return carry

    lax.fori_loop(1, line, step, 0)

    for part in tops:
        for q in range(top_line):
            device = part.base + q * GROUP1 + lax.rem(xpeer, GROUP1)
            part.arrived(device, me)
            part.copy(device, cpeer, part.core).start()
    for part in (root,) + tops:
        def other(q, carry):
            for peer in (cpeer, cpeer + xpeer - me):
                part.arrived(part.base + q * GROUP1 + lax.rem(peer, GROUP1), me)
            return carry

        lax.fori_loop(0, part.group // GROUP1, other, 0)
        part.keep(me).wait()

    for part in mids:
        part.arrived(xpeer, me)
        part.copy(xpeer, cpeer, part.core).start()
    for part in mids:
        part.arrived(cpeer, me)
        part.arrived(cpeer + xpeer - me, me)
        part.keep(me).wait()

    own_copies(wait_send)
    along(root, xpeer, True, has_up, wait_send)
    along(root, xpeer, False, has_down, wait_send)
    root.copy(xpeer, cpeer, root.core).wait_send()

    def drain(s, carry):
        for go_up in (True, False):
            shift = -s * GROUP1 if go_up else s * GROUP1
            got_top = (top_place >= s) if go_up else (top_place + s < top_line)
            got_root = (place >= s) if go_up else (place + s < line)

            @pl.when(got_top)
            def _():
                for part in tops:
                    along(part, me + shift, go_up, top_up if go_up else top_down, wait_send)
                    part.copy(me + shift, xpeer, part.side).wait_send()
                    part.copy(me + shift, cpeer, part.core).wait_send()

            @pl.when(got_root)
            def _():
                for device in (me, xpeer):
                    along(root, device + shift, go_up, has_up if go_up else has_down, wait_send)
                    root.copy(device + shift, cpeer, root.core).wait_send()

        return carry

    lax.fori_loop(1, line, drain, 0)
    for part in tops:
        for q in range(top_line):
            device = part.base + q * GROUP1 + lax.rem(xpeer, GROUP1)
            part.copy(device, cpeer, part.core).wait_send()
    for part in mids:
        part.copy(xpeer, cpeer, part.core).wait_send()


def tree_kernel(
    place_ref,
    top_columns,
    mid_columns,
    leaf_columns,
    top_pattern,
    mid_parent,
    leaf_parent,
    mid_pattern,
    leaf_pattern,
    leaf_live,
    root_all,
    tl_all,
    td_all,
    ml_all,
    md_all,
    leaf_lhat,
    leaf_dinv,
    top_diag_out,
    top_coup_out,
    mid_diag_out,
    mid_coup_out,
    leaf_diag_out,
    leaf_coup_out,
    e0h,
    e0l,
    e2h,
    e2l,
    e1h,
    e1l,
    lcat,
    ccat,
    top_c,
    top_d,
):
    me = place_ref[0]
    cols = leaf_dinv.shape[2]
    frame = SLOTS * cols

    per = root_all.shape[1] // cols
    for a in range(per):
        for b in range(per):
            high, low = split(root_all[a * cols : (a + 1) * cols, b * cols : (b + 1) * cols])
            e0h[0, a, b] = high
            e0l[0, a, b] = low

    row_ids = lax.broadcasted_iota(jnp.int32, (cols, cols), 0)
    lane_ids = lax.broadcasted_iota(jnp.int32, (cols, cols), 1)

    def solve(src_h, src_l, source, pattern, lhat, dinv, used, put_coup, put_diag, dst=None):
        keep = lane_ids < used
        for r in range(SLOTS):
            high, low = split(jnp.where(keep, lhat(r), 0.0))
            lcat[r * cols : (r + 1) * cols] = high
            lcat[frame + r * cols : frame + (r + 1) * cols] = low
            lcat[2 * frame + r * cols : 2 * frame + (r + 1) * cols] = high
        for r in range(SLOTS):
            highs = [src_h[source, pattern[r], pattern[k]] for k in range(SLOTS)]
            lows = [src_l[source, pattern[r], pattern[k]] for k in range(SLOTS)]
            wide = jnp.concatenate(highs + highs + lows, axis=1)
            coup = -jnp.dot(wide, lcat[...], preferred_element_type=f32)
            put_coup(r, coup)
            high, low = split(coup)
            ccat[r * cols : (r + 1) * cols] = high
            ccat[frame + r * cols : frame + (r + 1) * cols] = high
            ccat[2 * frame + r * cols : 2 * frame + (r + 1) * cols] = low
            if dst is not None:
                dst_h, dst_l, place_at = dst
                dst_h[place_at, r + 1, 0] = high
                dst_l[place_at, r + 1, 0] = low
                high, low = split(coup.T)
                dst_h[place_at, 0, r + 1] = high
                dst_l[place_at, 0, r + 1] = low
                for k in range(SLOTS):
                    dst_h[place_at, r + 1, k + 1] = highs[k]
                    dst_l[place_at, r + 1, k + 1] = lows[k]
        product = lax.dot_general(
            lcat[...], ccat[...], (((0,), (0,)), ((), ())), preferred_element_type=f32
        )
        diag = jnp.where(keep & (row_ids < used), dinv, 0.0) - product
        put_diag(diag)
        if dst is not None:
            high, low = split(diag)
            dst_h[place_at, 0, 0] = high
            dst_l[place_at, 0, 0] = low

    top_base = me // GROUP2 * NODES2

    def top_step(q, carry):
        pattern = [top_pattern[top_base + q, k] for k in range(SLOTS)]

        def lhat(r):
            return tl_all[pl.ds(pl.multiple_of(q * frame + r * cols, cols), cols)]

        def put_coup(r, value):
            top_c[pl.ds(pl.multiple_of(q * frame + r * cols, cols), cols)] = value

        def put_diag(value):
            top_d[pl.ds(pl.multiple_of(q * cols, cols), cols)] = value

        dinv = td_all[pl.ds(pl.multiple_of(q * cols, cols), cols)]
        used = top_columns[top_base + q]
        solve(e0h, e0l, 0, pattern, lhat, dinv, used, put_coup, put_diag, (e2h, e2l, q))
        return carry

    lax.fori_loop(0, NODES2, top_step, 0)
    member = lax.rem(me, GROUP2)
    rows = top_coup_out.shape[0]
    top_coup_out[...] = top_c[pl.ds(pl.multiple_of(member * rows, 8), rows)]
    rows = top_diag_out.shape[0]
    top_diag_out[...] = top_d[pl.ds(pl.multiple_of(member * rows, 8), rows)]

    leaves = leaf_lhat.shape[0]
    mid_base = me // GROUP1 * GROUP1

    def mid_step(step_index, carry):
        k = leaves - step_index
        leaf = me * leaves + jnp.maximum(k - 1, 0)
        local = jnp.where(k == 0, lax.rem(me, GROUP1), leaf_parent[leaf] - mid_base)
        node = mid_base + local
        pattern = [mid_pattern[node, s] for s in range(SLOTS)]

        def lhat(r):
            return ml_all[pl.ds(pl.multiple_of(local * frame + r * cols, cols), cols)]

        def put_coup(r, value):
            mid_coup_out[r * cols : (r + 1) * cols] = value

        def put_diag(value):
            mid_diag_out[...] = value

        dinv = md_all[pl.ds(pl.multiple_of(local * cols, cols), cols)]
        source = mid_parent[node] - top_base
        solve(
            e2h, e2l, source, pattern, lhat, dinv, mid_columns[node], put_coup, put_diag,
            (e1h, e1l, k),
        )
        return carry

    lax.fori_loop(0, leaves + 1, mid_step, 0)

    def leaf_step(i, carry):
        node = me * leaves + i
        pattern = [leaf_pattern[node, s] for s in range(SLOTS)]
        live = jnp.full((cols, cols), i, jnp.int32) < leaf_live[me]

        def lhat(r):
            return leaf_lhat[i, r * cols : (r + 1) * cols]

        def put_coup(r, value):
            leaf_coup_out[i, r * cols : (r + 1) * cols] = jnp.where(live, value, 0.0)

        def put_diag(value):
            leaf_diag_out[i] = jnp.where(live, value, 0.0)

        solve(e1h, e1l, i + 1, pattern, lhat, leaf_dinv[i], leaf_columns[node], put_coup, put_diag)
        return carry

    lax.fori_loop(0, leaves, leaf_step, 0)


def body(
    root_frame,
    top_lhat,
    top_dinv,
    mid_lhat,
    mid_dinv,
    leaf_lhat,
    leaf_dinv,
    *scalars,
):
    n = lax.axis_size("leaf")
    cols = top_dinv.shape[1]
    frame = SLOTS * cols
    per = root_frame.shape[1] // cols
    leaves = leaf_lhat.shape[0]
    grid = SLOTS + 1

    def dma(count):
        return pltpu.SemaphoreType.DMA((count,))

    sems = []
    for group in (n, GROUP2, GROUP2, GROUP1, GROUP1):
        sems += [dma(group) for _ in range(5)] + [dma(1)]
    vmem = pl.BlockSpec(memory_space=pltpu.VMEM)
    smem = pl.BlockSpec(memory_space=pltpu.SMEM)
    anywhere = pl.BlockSpec(memory_space=pl.ANY)
    mine = (root_frame, top_lhat, top_dinv, mid_lhat[0], mid_dinv[0])
    groups = (n, GROUP2, GROUP2, GROUP1, GROUP1)
    whole = pl.pallas_call(
        functools.partial(gather_kernel, n),
        out_shape=[
            jax.ShapeDtypeStruct((count * x.shape[0], x.shape[1]), f32)
            for count, x in zip(groups, mine)
        ],
        in_specs=[anywhere] * 5,
        out_specs=[anywhere] * 5,
        scratch_shapes=sems,
        compiler_params=pltpu.CompilerParams(
            collective_id=0, has_side_effects=True, vmem_limit_bytes=1024 * 1024
        ),
    )(*mine)
    outs = pl.pallas_call(
        tree_kernel,
        out_shape=[
            jax.ShapeDtypeStruct(top_dinv.shape, f32),
            jax.ShapeDtypeStruct(top_lhat.shape, f32),
            jax.ShapeDtypeStruct(mid_dinv.shape[1:], f32),
            jax.ShapeDtypeStruct(mid_lhat.shape[1:], f32),
            jax.ShapeDtypeStruct(leaf_dinv.shape, f32),
            jax.ShapeDtypeStruct(leaf_lhat.shape, f32),
        ],
        in_specs=[smem] * 10 + [vmem] * 7,
        out_specs=[vmem] * 6,
        scratch_shapes=[
            pltpu.VMEM((1, per, per, cols, cols), bf16),
            pltpu.VMEM((1, per, per, cols, cols), bf16),
            pltpu.VMEM((NODES2, grid, grid, cols, cols), bf16),
            pltpu.VMEM((NODES2, grid, grid, cols, cols), bf16),
            pltpu.VMEM((leaves + 1, grid, grid, cols, cols), bf16),
            pltpu.VMEM((leaves + 1, grid, grid, cols, cols), bf16),
            pltpu.VMEM((3 * frame, cols), bf16),
            pltpu.VMEM((3 * frame, cols), bf16),
            pltpu.VMEM((NODES2 * frame, cols), f32),
            pltpu.VMEM((NODES2 * cols, cols), f32),
        ],
        compiler_params=pltpu.CompilerParams(vmem_limit_bytes=36 * 1024 * 1024),
    )(lax.axis_index("leaf").reshape(1).astype(jnp.int32), *scalars, *whole, leaf_lhat, leaf_dinv)
    return (outs[0], outs[1], outs[2][None], outs[3][None], outs[4], outs[5])


def solution(mesh):
    rows = P(("pole", "leaf"), None)
    stacks = P(("pole", "leaf"), None, None)
    in_specs = (rows,) * 3 + (stacks,) * 4 + (P(),) * 9
    out_specs = (rows,) * 2 + (stacks,) * 4
    return jax.shard_map(body, mesh=mesh, in_specs=in_specs, out_specs=out_specs, check_vma=False)
```

time: 485 us -> 85.1 us (0.18)
  the two profiles are of different devices: /device:TPU:3 before, /device:TPU:0 now
where the time goes in v1:
time: 85.1 us; the launch traced here: 84.6 us
  Pallas kernels  71.8 us (84%)
  local copies, waits for them, and re-layouts  12.2 us (14%)
    pallas_call x1, Pallas kernels, body(): pl.pallas_call(functools.partial(gather_kernel, n), out_shape=[jax.ShapeD...  54.4 us
    pallas_call x1, Pallas kernels, body(): pl.pallas_call(tree_kernel, out_shape=[jax.ShapeDtypeStruct(top_dinv.shap...  17.4 us
    unnamed x30, local copies, waits for them, and re-layouts  12.2 us

profile of v1, /device:TPU:0, one launch (start us, length us, event | category | flops | bytes accessed | tf_op | source)
XLA Modules:
  0.0 84.6 jit_solution(18297855407175419177)
XLA Ops:
  0.6 0.8 copy.22.mid_pattern
  1.4 0.8 copy.23.leaf_pattern
  2.2 0.0 copy-start.1
  2.2 1.1 %copy-done.1 = f32[1,768,256]{2,1,0:T(8,128)S(1)} copy-done((f32[1,768,256]{2,1,0:T(8,128)S(1)}, f32[1,768,256]{2,1,0:T(8,128)}, u32[]{:S(2)}) %copy-start.1) | copy-done | bytes 786456
  3.3 0.0 copy-start.3
  3.3 0.9 %copy-done.3 = f32[64,1024]{1,0:T(8,128)S(1)} copy-done((f32[64,1024]{1,0:T(8,128)S(1)}, f32[64,1024]{1,0:T(8,128)}, u32[]{:S(2)}) %copy-start.3) | copy-done | bytes 262168
  4.2 0.0 copy-start.4
  4.2 0.9 %copy-done.4 = f32[1,256,256]{2,1,0:T(8,128)S(1)} copy-done((f32[1,256,256]{2,1,0:T(8,128)S(1)}, f32[1,256,256]{2,1,0:T(8,128)}, u32[]{:S(2)}) %copy-start.4) | copy-done | bytes 262168
  5.2 0.0 copy-start.5
  5.2 0.9 %copy-done.5 = f32[96,256]{1,0:T(8,128)S(1)} copy-done((f32[96,256]{1,0:T(8,128)S(1)}, f32[96,256]{1,0:T(8,128)}, u32[]{:S(2)}) %copy-start.5) | copy-done | bytes 98328
  6.1 0.0 copy-start.6
  6.1 0.8 copy-done.6
  6.8 0.0 copy-start.2
  6.8 54.4 %shard_map.199 = (f32[1024,1024]{1,0:T(8,128)S(1)}, f32[1536,256]{1,0:T(8,128)S(1)}, f32[512,256]{1,0:T(8,128)S(1)}, f32[3072,256]{1,0:T(8,128)S(1)}, f32[1024,256]{1,0:T(8,128)S(1)}) custom-call(f32[64,1024]{1,0:T(8,128)S(1)} %copy-done.3, f32[96,256]{1,0:T(8,128)S(1)} %copy-done.5, f32[32,256]{1,0:T(8,128)S(1)} %copy-done.6, f32[768,256]{1,0:T(8,128)S(1)} %bitcast.5, ...), custom_call_target="tpu_custom_call" | custom-call | tf_op jit(solution)/shard_map/pallas_call | solution.py:428
  61.2 0.0 copy-done.2
  61.2 0.0 copy-start
  61.2 1.4 %copy-done = f32[2,768,256]{2,1,0:T(8,128)S(1)} copy-done((f32[2,768,256]{2,1,0:T(8,128)S(1)}, f32[2,768,256]{2,1,0:T(8,128)}, u32[]{:S(2)}) %copy-start) | copy-done | bytes 1572888
  62.6 0.0 copy-start.7
  62.6 0.7 copy-done.7
  63.3 0.0 copy-start.8
  63.3 0.7 copy-done.8
  64.0 0.0 copy-start.9
  64.0 0.7 copy-done.9
  64.6 0.0 copy-start.10
  64.6 0.7 copy-done.10
  65.3 0.0 copy-start.11
  65.3 0.7 copy-done.11
  65.9 0.0 copy-start.12
  65.9 0.7 copy-done.12
  66.6 0.0 copy-start.13
  66.6 0.7 copy-done.13
  67.3 17.4 %shard_map.200 = (f32[32,256]{1,0:T(8,128)}, f32[96,256]{1,0:T(8,128)}, f32[256,256]{1,0:T(8,128)}, f32[768,256]{1,0:T(8,128)}, f32[2,256,256]{2,1,0:T(8,128)}, /*index=5*/f32[2,768,256]{2,1,0:T(8,128)}) custom-call(s32[1]{0:T(128)} %bitcast.place_ref, s32[2]{0:T(128)S(1)} %copy-done.8, s32[16]{0:T(128)S(1)} %copy-done.9, s32[32]{0:T(128)S(1)} %copy-done.10, ...), custom_call_target="tpu_custom_call" | custom-call | tf_op jit(solution)/shard_map/pallas_call | solution.py:441
Async XLA Ops:
  2.2 1.1 %copy-start.1 = (f32[1,768,256]{2,1,0:T(8,128)S(1)}, f32[1,768,256]{2,1,0:T(8,128)}, u32[]{:S(2)}) copy-start(f32[1,768,256]{2,1,0:T(8,128)} %param.19) | copy-start | bytes 2359300
  3.3 0.9 %copy-start.3 = (f32[64,1024]{1,0:T(8,128)S(1)}, f32[64,1024]{1,0:T(8,128)}, u32[]{:S(2)}) copy-start(f32[64,1024]{1,0:T(8,128)} %root_in.1) | copy-start | bytes 786436
  4.2 0.9 %copy-start.4 = (f32[1,256,256]{2,1,0:T(8,128)S(1)}, f32[1,256,256]{2,1,0:T(8,128)}, u32[]{:S(2)}) copy-start(f32[1,256,256]{2,1,0:T(8,128)} %param.20) | copy-start | bytes 786436
  5.2 0.9 %copy-start.5 = (f32[96,256]{1,0:T(8,128)S(1)}, f32[96,256]{1,0:T(8,128)}, u32[]{:S(2)}) copy-start(f32[96,256]{1,0:T(8,128)} %tl_in.1) | copy-start | bytes 294916
  6.1 0.8 copy-start.6
  6.8 54.4 %copy-start.2 = (f32[2,256,256]{2,1,0:T(8,128)S(1)}, f32[2,256,256]{2,1,0:T(8,128)}, u32[]{:S(2)}) copy-start(f32[2,256,256]{2,1,0:T(8,128)} %leaf_dinv.1) | copy-start | bytes 1572868
  61.2 1.4 %copy-start = (f32[2,768,256]{2,1,0:T(8,128)S(1)}, f32[2,768,256]{2,1,0:T(8,128)}, u32[]{:S(2)}) copy-start(f32[2,768,256]{2,1,0:T(8,128)} %leaf_lhat.1) | copy-start | bytes 4718596
  62.6 0.7 copy-start.7
  63.3 0.7 copy-start.8
  64.0 0.7 copy-start.9
  64.6 0.7 copy-start.10
  65.3 0.7 copy-start.11
  65.9 0.7 copy-start.12
  66.6 0.7 copy-start.13

commit v2 on v1

--- a/solution.py
+++ b/solution.py
@@ -34,9 +34,14 @@
     )
 
 
+def in_hbm(x):
+    return pltpu.with_memory_space_constraint(x, pltpu.HBM)
+
+
 class Spread:
-    def __init__(self, own, whole, group, sems, me):
+    def __init__(self, own, whole, group, sems, me, valid=None):
         self.own, self.whole, self.group = own, whole, group
+        self.valid = valid
         self.rows = own.shape[0]
         self.recv, self.up, self.down, self.side, self.core, self.local = sems
         self.base = me - lax.rem(me, group)
@@ -64,28 +69,48 @@
 
 def gather_kernel(
     n,
+    pieces,
     root_in,
     tl_in,
     td_in,
     ml_in,
     md_in,
-    root_all,
-    tl_all,
-    td_all,
-    ml_all,
-    md_all,
-    *sems,
+    *rest,
 ):
+    root_alls, rest = rest[:pieces], rest[pieces:]
+    tl_all, td_all, ml_all, md_all = rest[:4]
+    sems = rest[4:]
     me = lax.axis_index("leaf")
     core = lax.rem(me, 2)
     side = lax.rem(me // 2, 2)
     cpeer = me + 1 - 2 * core
     xpeer = me + 2 - 4 * side
-    root = Spread(root_in, root_all, n, sems[0:6], me)
-    tl = Spread(tl_in, tl_all, GROUP2, sems[6:12], me)
-    td = Spread(td_in, td_all, GROUP2, sems[12:18], me)
-    ml = Spread(ml_in, ml_all, GROUP1, sems[18:24], me)
-    md = Spread(md_in, md_all, GROUP1, sems[24:30], me)
+    cols = td_in.shape[1]
+    root_rows = root_in.shape[0]
+    per = root_in.shape[1] // cols
+    block_row = me * root_rows // cols
+
+    def in_half(device):
+        return device * root_rows // cols < per // 2
+
+    roots = []
+    for k in range(pieces):
+        column = pl.multiple_of(lax.rem(block_row + k, per) * cols, cols)
+        roots.append(
+            Spread(
+                root_in.at[:, pl.ds(column, cols)],
+                root_alls[k],
+                n,
+                sems[6 * k : 6 * k + 6],
+                me,
+                in_half if k == per // 2 else None,
+            )
+        )
+    sems = sems[6 * pieces :]
+    tl = Spread(tl_in, tl_all, GROUP2, sems[0:6], me)
+    td = Spread(td_in, td_all, GROUP2, sems[6:12], me)
+    ml = Spread(ml_in, ml_all, GROUP1, sems[12:18], me)
+    md = Spread(md_in, md_all, GROUP1, sems[18:24], me)
     tops = (tl, td)
     mids = (ml, md)
 
@@ -108,8 +133,16 @@
     def _():
         pl.semaphore_signal(barrier, inc=1, device_id={"leaf": me - GROUP1}, device_id_type=MESH)
 
-    for part in (root,) + tops + mids:
+    def when(part, device, act):
+        if part.valid is None:
+            act()
+        else:
+            pl.when(part.valid(device))(act)
+
+    for part in tops + mids:
         part.keep(me).start()
+    for part in roots:
+        when(part, me, lambda: part.keep(me).start())
     peers = 2 + jnp.minimum(place, 1) + jnp.minimum(line - 1 - place, 1)
     pl.semaphore_wait(barrier, peers)
 
@@ -132,16 +165,35 @@
     top_up = top_place < top_line - 1
     top_down = top_place > 0
 
+    def root_line(device, go_up, act, own=False):
+        for part in roots:
+            def go():
+                along(part, device, go_up, has_up if go_up else has_down, act, own)
+
+            when(part, device, go)
+
+    def root_to(device, target, core_way, act, own=False):
+        for part in roots:
+            def go():
+                act(part.copy(device, target, part.core if core_way else part.side, own))
+
+            when(part, device, go)
+
+    def root_arrived(device):
+        for part in roots:
+            when(part, device, lambda: part.arrived(device, me))
+
     def own_copies(act):
-        act(root.copy(me, xpeer, root.side, True))
+        root_to(me, xpeer, False, act, True)
         for part in tops:
             along(part, me, True, top_up, act, True)
             along(part, me, False, top_down, act, True)
-        along(root, me, True, has_up, act, True)
-        along(root, me, False, has_down, act, True)
+        root_line(me, True, act, True)
+        root_line(me, False, act, True)
         for part in tops:
             act(part.copy(me, xpeer, part.side, True))
-        for part in (root,) + tops:
+        root_to(me, cpeer, True, act, True)
+        for part in tops:
             act(part.copy(me, cpeer, part.core, True))
         for part in mids:
             act(part.copy(me, xpeer, part.side, True))
@@ -149,10 +201,10 @@
 
     own_copies(start)
 
-    root.arrived(xpeer, me)
-    along(root, xpeer, True, has_up, start)
-    along(root, xpeer, False, has_down, start)
-    root.copy(xpeer, cpeer, root.core).start()
+    root_arrived(xpeer)
+    root_line(xpeer, True, start)
+    root_line(xpeer, False, start)
+    root_to(xpeer, cpeer, True, start)
 
     def step(s, carry):
         for go_up in (True, False):
@@ -171,9 +223,9 @@
             @pl.when(got_root)
             def _():
                 for device in (me, xpeer):
-                    root.arrived(device + shift, me)
-                    along(root, device + shift, go_up, has_up if go_up else has_down, start)
-                    root.copy(device + shift, cpeer, root.core).start()
+                    root_arrived(device + shift)
+                    root_line(device + shift, go_up, start)
+                    root_to(device + shift, cpeer, True, start)
 
         return carry
 
@@ -184,14 +236,15 @@
             device = part.base + q * GROUP1 + lax.rem(xpeer, GROUP1)
             part.arrived(device, me)
             part.copy(device, cpeer, part.core).start()
-    for part in (root,) + tops:
+    for part in tuple(roots) + tops:
         def other(q, carry):
             for peer in (cpeer, cpeer + xpeer - me):
-                part.arrived(part.base + q * GROUP1 + lax.rem(peer, GROUP1), me)
+                device = part.base + q * GROUP1 + lax.rem(peer, GROUP1)
+                when(part, device, lambda: part.arrived(device, me))
             return carry
 
         lax.fori_loop(0, part.group // GROUP1, other, 0)
-        part.keep(me).wait()
+        when(part, me, lambda: part.keep(me).wait())
 
     for part in mids:
         part.arrived(xpeer, me)
@@ -202,9 +255,9 @@
         part.keep(me).wait()
 
     own_copies(wait_send)
-    along(root, xpeer, True, has_up, wait_send)
-    along(root, xpeer, False, has_down, wait_send)
-    root.copy(xpeer, cpeer, root.core).wait_send()
+    root_line(xpeer, True, wait_send)
+    root_line(xpeer, False, wait_send)
+    root_to(xpeer, cpeer, True, wait_send)
 
     def drain(s, carry):
         for go_up in (True, False):
@@ -222,8 +275,8 @@
             @pl.when(got_root)
             def _():
                 for device in (me, xpeer):
-                    along(root, device + shift, go_up, has_up if go_up else has_down, wait_send)
-                    root.copy(device + shift, cpeer, root.core).wait_send()
+                    root_line(device + shift, go_up, wait_send)
+                    root_to(device + shift, cpeer, True, wait_send)
 
         return carry
 
@@ -236,51 +289,40 @@
         part.copy(xpeer, cpeer, part.core).wait_send()
 
 
-def tree_kernel(
-    place_ref,
-    top_columns,
-    mid_columns,
-    leaf_columns,
-    top_pattern,
-    mid_parent,
-    leaf_parent,
-    mid_pattern,
-    leaf_pattern,
-    leaf_live,
-    root_all,
-    tl_all,
-    td_all,
-    ml_all,
-    md_all,
-    leaf_lhat,
-    leaf_dinv,
-    top_diag_out,
-    top_coup_out,
-    mid_diag_out,
-    mid_coup_out,
-    leaf_diag_out,
-    leaf_coup_out,
-    e0h,
-    e0l,
-    e2h,
-    e2l,
-    e1h,
-    e1l,
-    lcat,
-    ccat,
-    top_c,
-    top_d,
-):
-    me = place_ref[0]
+def tree_kernel(pieces, *refs):
+    small_in, mid_pattern, leaf_pattern = refs[:7], refs[7], refs[8]
+    root_alls, refs = refs[9 : 9 + pieces], refs[9 + pieces :]
+    tl_all, td_all, ml_all, md_all, leaf_lhat_in, leaf_dinv_in = refs[:6]
+    (
+        top_diag_out,
+        top_coup_out,
+        mid_diag_out,
+        mid_coup_out,
+        leaf_diag_out,
+        leaf_coup_out,
+    ) = refs[6:12]
+    e0h, e0l, e2h, e2l, e1h, e1l, lcat, ccat, top_c, top_d, leaf_lhat, leaf_dinv = refs[12:24]
+    small = refs[24:31]
+    sems = refs[31]
+    top_columns, mid_columns, leaf_columns, top_pattern, mid_parent, leaf_parent, leaf_live = small
+    fetched = list(zip(small_in + (leaf_lhat_in, leaf_dinv_in), small + (leaf_lhat, leaf_dinv)))
+    fetches = [pltpu.make_async_copy(a, b, sems.at[i]) for i, (a, b) in enumerate(fetched)]
+    for fetch in fetches:
+        fetch.start()
+    me = lax.axis_index("leaf")
     cols = leaf_dinv.shape[2]
     frame = SLOTS * cols
 
-    per = root_all.shape[1] // cols
-    for a in range(per):
-        for b in range(per):
-            high, low = split(root_all[a * cols : (a + 1) * cols, b * cols : (b + 1) * cols])
-            e0h[0, a, b] = high
-            e0l[0, a, b] = low
+    per = e0h.shape[1]
+    for k in range(pieces):
+        for a in range(per // 2 if k == per // 2 else per):
+            b = (a + k) % per
+            value = root_alls[k][a * cols : (a + 1) * cols]
+            e0h[0, a, b], e0l[0, a, b] = split(value)
+            if k:
+                e0h[0, b, a], e0l[0, b, a] = split(value.T)
+    for fetch in fetches[:-2]:
+        fetch.wait()
 
     row_ids = lax.broadcasted_iota(jnp.int32, (cols, cols), 0)
     lane_ids = lax.broadcasted_iota(jnp.int32, (cols, cols), 1)
@@ -377,6 +419,9 @@
 
     lax.fori_loop(0, leaves + 1, mid_step, 0)
 
+    for fetch in fetches[-2:]:
+        fetch.wait()
+
     def leaf_step(i, carry):
         node = me * leaves + i
         pattern = [leaf_pattern[node, s] for s in range(SLOTS)]
@@ -417,29 +462,38 @@
     def dma(count):
         return pltpu.SemaphoreType.DMA((count,))
 
+    pieces = per // 2 + 1
     sems = []
-    for group in (n, GROUP2, GROUP2, GROUP1, GROUP1):
+    for group in (n,) * pieces + (GROUP2, GROUP2, GROUP1, GROUP1):
         sems += [dma(group) for _ in range(5)] + [dma(1)]
     vmem = pl.BlockSpec(memory_space=pltpu.VMEM)
     smem = pl.BlockSpec(memory_space=pltpu.SMEM)
     anywhere = pl.BlockSpec(memory_space=pl.ANY)
     mine = (root_frame, top_lhat, top_dinv, mid_lhat[0], mid_dinv[0])
-    groups = (n, GROUP2, GROUP2, GROUP1, GROUP1)
+    groups = (GROUP2, GROUP2, GROUP1, GROUP1)
+    root_rows = n * root_frame.shape[0]
+    root_shapes = [
+        jax.ShapeDtypeStruct((root_rows // 2 if k == per // 2 else root_rows, cols), f32)
+        for k in range(pieces)
+    ]
+    hbm = pl.BlockSpec(memory_space=pltpu.HBM)
     whole = pl.pallas_call(
-        functools.partial(gather_kernel, n),
-        out_shape=[
+        functools.partial(gather_kernel, n, pieces),
+        out_shape=root_shapes
+        + [
             jax.ShapeDtypeStruct((count * x.shape[0], x.shape[1]), f32)
-            for count, x in zip(groups, mine)
+            for count, x in zip(groups, mine[1:])
         ],
-        in_specs=[anywhere] * 5,
-        out_specs=[anywhere] * 5,
+        in_specs=[hbm] * 5,
+        out_specs=[anywhere] * (pieces + 4),
         scratch_shapes=sems,
         compiler_params=pltpu.CompilerParams(
             collective_id=0, has_side_effects=True, vmem_limit_bytes=1024 * 1024
         ),
-    )(*mine)
+    )(*[in_hbm(x) for x in mine])
+    small = scalars[:6] + scalars[8:]
     outs = pl.pallas_call(
-        tree_kernel,
+        functools.partial(tree_kernel, pieces),
         out_shape=[
             jax.ShapeDtypeStruct(top_dinv.shape, f32),
             jax.ShapeDtypeStruct(top_lhat.shape, f32),
@@ -448,7 +502,7 @@
             jax.ShapeDtypeStruct(leaf_dinv.shape, f32),
             jax.ShapeDtypeStruct(leaf_lhat.shape, f32),
         ],
-        in_specs=[smem] * 10 + [vmem] * 7,
+        in_specs=[hbm] * 7 + [smem] * 2 + [vmem] * (pieces + 4) + [hbm] * 2,
         out_specs=[vmem] * 6,
         scratch_shapes=[
             pltpu.VMEM((1, per, per, cols, cols), bf16),
@@ -461,9 +515,15 @@
             pltpu.VMEM((3 * frame, cols), bf16),
             pltpu.VMEM((NODES2 * frame, cols), f32),
             pltpu.VMEM((NODES2 * cols, cols), f32),
-        ],
+            pltpu.VMEM(leaf_lhat.shape, f32),
+            pltpu.VMEM(leaf_dinv.shape, f32),
+        ]
+        + [pltpu.SMEM(x.shape, jnp.int32) for x in small]
+        + [dma(len(small) + 2)],
         compiler_params=pltpu.CompilerParams(vmem_limit_bytes=36 * 1024 * 1024),
-    )(lax.axis_index("leaf").reshape(1).astype(jnp.int32), *scalars, *whole, leaf_lhat, leaf_dinv)
+    )(
+        *[in_hbm(x) for x in small], scalars[6], scalars[7], *whole, in_hbm(leaf_lhat), in_hbm(leaf_dinv)
+    )
     return (outs[0], outs[1], outs[2][None], outs[3][None], outs[4], outs[5])
 
 

time: 85.1 us -> 71.4 us (0.84)
  local copies, waits for them, and re-layouts: 12.2 us -> 1.52 us
  Pallas kernels: 71.8 us -> 69 us
    unnamed x30 -> x2, local copies, waits for them, and re-layouts: 12.2 us -> 1.52 us
    pallas_call x2, Pallas kernels: 71.8 us -> 69 us  [the longest x1 50.8 us: body(): pl.pallas_call(functools.partial(gather_kernel, n, pieces), out_shape=roo...]
where the time goes in v2:
time: 71.4 us; the launch traced here: 71.2 us
  Pallas kernels  69 us (97%)
  local copies, waits for them, and re-layouts  1.52 us (2%)
    pallas_call x1, Pallas kernels, body(): pl.pallas_call(functools.partial(gather_kernel, n, pieces), out_shape=roo...  50.8 us
    pallas_call x1, Pallas kernels, body(): pl.pallas_call(functools.partial(tree_kernel, pieces), out_shape=[jax.Sha...  18.2 us
    unnamed x2, local copies, waits for them, and re-layouts  1.52 us

profile of v2, /device:TPU:0, one launch (start us, length us, event | category | flops | bytes accessed | tf_op | source)
XLA Modules:
  0.0 71.2 jit_solution(1971482971104572312)
XLA Ops:
  0.6 0.8 %copy.22.refs_7_ = s32[16,3]{1,0:T(8,128)S(1)} copy(s32[16,3]{0,1:T(4,128)} %param.29) | data formatting | bytes 384 | tf_op args[13]
  1.4 0.8 %copy.23.refs_8_ = s32[32,3]{1,0:T(8,128)S(1)} copy(s32[32,3]{0,1:T(4,128)} %param.30) | data formatting | bytes 768 | tf_op args[14]
  2.2 50.8 %shard_map.199 = (f32[1024,256]{1,0:T(8,128)S(1)}, f32[1024,256]{1,0:T(8,128)S(1)}, f32[512,256]{1,0:T(8,128)S(1)}, f32[1536,256]{1,0:T(8,128)S(1)}, f32[512,256...) custom-call(f32[64,1024]{1,0:T(8,128)} %root_in.1, f32[96,256]{1,0:T(8,128)} %tl_in.1, ...), custom_call_target="tpu_custom_call" | custom-call | tf_op jit(solution)/shard_map/pallas_call | solution.py:480
  52.9 18.2 %shard_map.200 = (f32[32,256]{1,0:T(8,128)}, f32[96,256]{1,0:T(8,128)}, f32[256,256]{1,0:T(8,128)}, f32[768,256]{1,0:T(8,128)}, f32[2,256,256]{2,1,0:T(8,128)}, /*index=5*/f32[2,768,256]{2,1,0:T(8,128)}) custom-call(s32[2]{0:T(128)} %refs_0_.1, s32[16]{0:T(128)} %refs_1_.1, s32[32]{0:T(128)} %refs_2_.1, s32[2,3]{1,0:T(2,128)} %refs_3_.1, s32[16]{0:T(128)} %refs_4_.1, ...), custom_call_target="tpu_custom_call" | custom-call | tf_op jit(solution)/shard_map/pallas_call | solution.py:495
